TPU v7x, 32 devices: a whole 2x2x4 slice. The times are simulated.
32 devices in a mesh: pts: 8 (over z, y), hrs: 4 (over x, core).
Axes of the slice: x: 2, y: 2, z: 4, core: 2. Of those that a mesh axis runs over, the one named last changes fastest.
Arguments:
- fields: float32 [512, 65536], P(('pts', 'hrs')), may hold values from -2000 to 2000, as said below
- probes: float32 [256, 512], replicated, may hold values from -0.25 to 0.25
Outputs:
- basis_rows: float32 [256, 65536], P(None, ('pts', 'hrs'))
- coeffs: float32 [256, 512], replicated
Inputs may be any that keep to these rules, and one draw needn't show every extreme that they name: `fields`: every hour and every grid point carries its own scale, and the values are real-valued and never all zero.
All inputs are finite; a program needn't handle non-finite values.
Results may differ from a plain program's by a relative error of at most 0.00017.
Values sent between devices are 32-bit elements; how exact they have to be, the bound alone decides.
A program may use at most 64 MiB of HBM per device.

v0:
```python
import jax
import jax.numpy as jnp
from jax import lax
from jax.sharding import PartitionSpec as P

highest = lax.Precision.HIGHEST


def contract_last(left, right):
    return lax.dot_general(
        left, right, (((1,), (1,)), ((), ())), precision=highest, preferred_element_type=jnp.float32
    )


def on_device(fields, probes):
    n_pts = lax.axis_size("pts")
    n_hrs = lax.axis_size("hrs")
    panels = lax.all_to_all(fields, ("pts", "hrs"), split_axis=1, concat_axis=0, tiled=True)
    n_points = panels.shape[1] * n_pts * n_hrs
    sketched = jnp.dot(probes, panels, precision=highest, preferred_element_type=jnp.float32)
    cross_sum = lax.psum(contract_last(sketched, panels) / n_points, ("pts", "hrs"))
    local_gram = contract_last(sketched, sketched) / n_points
    gram_sum = lax.psum(local_gram, ("pts", "hrs"))
    factor = jnp.linalg.cholesky(gram_sum)
    basis_rows = lax.linalg.triangular_solve(factor, sketched, left_side=True, lower=True)
    coeffs = lax.linalg.triangular_solve(factor, cross_sum, left_side=True, lower=True)
    return (basis_rows, coeffs)


def solution(mesh):
    return jax.shard_map(
        on_device,
        mesh=mesh,
        in_specs=(P(("pts", "hrs"), None), P()),
        out_specs=(P(None, ("pts", "hrs")), P()),
        check_vma=False,
    )
```

profile of v0, /device:TPU:0, one launch (start us, length us, event | category | flops | bytes accessed | tf_op | source)
XLA Modules:
  0.0 328.4 jit_solution(12238962326394786213)
XLA Ops:
  7.2 2.5 copy.17
  9.7 100.7 %all_to_all.19 = f32[16,32,2048]{2,0,1:T(8,128)S(1)} all-to-all(f32[16,32,2048]{2,0,1:T(8,128)S(1)} %bitcast.50), channel_id=1, replica_groups=mesh['pts'=8,'hrs'=4] {'pts','hrs'}, dimensions={1} | all-to-all | bytes 8388608 | tf_op jit(solution)/shard_map/all_to_all | solution.py:18
  110.5 3.7 %fusion.13 = f32[256,2048]{1,0:T(8,128)S(1)} fusion(f32[256,512]{1,0:T(8,128)S(1)} %copy-done, f32[512,2048]{1,0:T(8,128)S(1)} %bitcast.48), kind=kOutput, calls=%fused_computation.38 | convolution fusion | flops 3221225472 | bytes 6815744 | tf_op jit(solution)/shard_map/dot_general | solution.py:20
  114.2 4.5 %convolution_multiply_fusion = f32[256,512]{1,0:T(8,128)} fusion(f32[256,2048]{1,0:T(8,128)S(1)} %fusion.13, f32[512,2048]{1,0:T(8,128)S(1)} %bitcast.49), kind=kOutput, calls=%fused_computation.5 | convolution fusion | flops 3221356544 | bytes 6815744 | tf_op jit(solution)/shard_map/dot_general | solution.py:10
  118.7 2.6 convolution_multiply_fusion.1
  121.3 129.5 %all-reduce.4.cloned.1.call-done = (f32[256,256]{0,1:T(8,128)}, f32[256,512]{1,0:T(8,128)}) async-done(((f32[256,256]{0,1:T(8,128)}, f32[256,512]{1,0:T(8,128)}), (f32[256,256]{0,1:T(8,128)}, f32[256,512]{1,0:T(8,128)})) %all-reduce.4.cloned.1.call-update) | async-done | bytes 786448 | tf_op jit(solution)/shard_map/psum | solution.py:23
  250.9 1.1 copy.13
  252.0 1.0 fusion.4
  253.0 11.9 %cholesky.50 = f32[128,128]{1,0:T(8,128)S(1)} custom-call(f32[128,128]{1,0:T(8,128)S(1)} %cholesky.118), custom_call_target="Cholesky" | custom-call | tf_op jit(solution)/shard_map/jit(cholesky)/cholesky | solution.py:24
  264.9 9.8 %custom-call.16 = f32[1,128,128]{1,2,0:T(8,128)S(1)} custom-call(f32[1,128,128]{2,1,0:T(8,128)S(1)} %get-tuple-element.25), custom_call_target="InvertDiagBlocksLowerTriangular" | custom-call | tf_op jit(solution)/shard_map/jit(cholesky)/cholesky | solution.py:24
  275.2 11.7 %cholesky.105 = f32[128,128]{1,0:T(8,128)S(1)} custom-call(f32[128,128]{1,0:T(8,128)S(1)} %convolution_subtract_fusion.2), custom_call_target="Cholesky" | custom-call | tf_op jit(solution)/shard_map/jit(cholesky)/cholesky | solution.py:24
  287.0 0.6 compare_reduce_fusion
  289.0 4.0 %while.1 = (s32[]{:T(128)}, f32[256,256]{1,0:T(8,128)S(1)}, s32[2,2]{1,0:T(2,128)S(1)}, f32[2,128,128]{2,1,0:T(8,128)S(1)}, s32[]{:T(128)}) while((s32[]{:T(128)}, f32[256,256]{1,0:T(8,128)S(1)}, s32[2,2]{1,0:T(2,128)S(1)}, f32[2,128,128]{2,1,0:T(8,128)S(1)}, s32[]{:T(128)}) %tuple.27), condition=%wide.while_cond, body=%wide.while_body.sunk | while | flops 2 | bytes 131181 | solution.py:25
  289.0 0.6 fusion.27
  289.6 1.4 bitcast_dynamic-update-slice_fusion.2
  291.6 1.4 bitcast_dynamic-update-slice_fusion.2
  293.0 19.9 %custom-call.17 = f32[2,128,128]{1,2,0:T(8,128)S(1)} custom-call(f32[2,128,128]{2,1,0:T(8,128)S(1)} %get-tuple-element.9), custom_call_target="InvertDiagBlocksLowerTriangular" | custom-call | tf_op jit(solution)/shard_map/triangular_solve | solution.py:25
  312.9 1.1 fusion
  314.0 1.4 fusion.2
  315.3 1.3 convolution_subtract_fusion.1
  317.1 0.8 pad_maximum_fusion.1
  317.9 1.0 convolution_subtract_fusion
  319.0 1.0 fusion.9
  320.0 1.5 pad_maximum_fusion
  (18 shorter events, 1.8 us)
Async XLA Ops:
  7.2 103.3 %copy-start = (f32[256,512]{1,0:T(8,128)S(1)}, f32[256,512]{1,0:T(8,128)}, u32[]{:S(2)}) copy-start(f32[256,512]{1,0:T(8,128)} %param.3) | copy-start | bytes 1572868
  7.2 243.7 %all-reduce.4.cloned.1.call-start = ((), (), s32[]{:S(2)}) async-start(), calls=%async_computation.1 | async-start | bytes 1572864 | tf_op jit(solution)/shard_map/psum | solution.py:23
Sparse Core Ops, SparseCore 0:
  121.4 129.3 all-reduce.3
where the time goes:
time: 329 us; the launch traced here: 328 us
  waiting for transfers between devices  130 us (40%)
  blocking collectives  101 us (31%)
  other arithmetic  57.4 us (17%)
  matrix products  17.5 us (5%)
  between operations  15.5 us (5%)
  local copies, waits for them, and re-layouts  7.64 us (2%)
    psum x1, waiting for transfers between devices, on_device(): gram_sum = lax.psum(local_gram, ('pts', 'hrs'))  130 us
    all_to_all x1, blocking collectives, on_device(): lax.all_to_all(fields, ('pts', 'hrs'), split_axis=1, concat_axis=0, tiled...  101 us
    another operation x6, other arithmetic, on_device(): factor = jnp.linalg.cholesky(gram_sum)  34.1 us
    another operation x4, other arithmetic, on_device(): lax.linalg.triangular_solve(factor, sketched, left_side=True, lower=True)  21.5 us
    dot_general x2, matrix products, contract_last(): lax.dot_general(left, right, (((1,), (1,)), ((), ())), precision=highest,...  7.09 us
  transfers between devices with their start and end apart: 1, of which 1 were waited for; matrix products, arithmetic and copies ran while one was open for 0% of the time, Pallas kernels for 0%

commit v1 on v0

--- a/solution.py
+++ b/solution.py
@@ -20,7 +20,7 @@
     sketched = jnp.dot(probes, panels, precision=highest, preferred_element_type=jnp.float32)
     cross_sum = lax.psum(contract_last(sketched, panels) / n_points, ("pts", "hrs"))
     local_gram = contract_last(sketched, sketched) / n_points
-    gram_sum = lax.psum(local_gram, ("pts", "hrs"))
+    gram_sum = lax.psum(lax.psum(local_gram, "hrs"), "pts")
     factor = jnp.linalg.cholesky(gram_sum)
     basis_rows = lax.linalg.triangular_solve(factor, sketched, left_side=True, lower=True)
     coeffs = lax.linalg.triangular_solve(factor, cross_sum, left_side=True, lower=True)

time: 329 us -> 372 us (1.13)
  waiting for transfers between devices: 130 us -> 170 us
    psum x1 -> x3, waiting for transfers between devices: 130 us -> 170 us  [the longest x2 98.9 us: on_device(): gram_sum = lax.psum(lax.psum(local_gram, 'hrs'), 'pts')]
  transfers between devices with their start and end apart: 1 -> 3, of which waited for: 1 -> 3; matrix products, arithmetic and copies ran while one was open for 0% -> 19% of each run, Pallas kernels for 0% -> 0%
where the time goes in v1:
time: 372 us
  waiting for transfers between devices  170 us (46%)
  blocking collectives  101 us (27%)
  other arithmetic  57.3 us (15%)
  matrix products  20.7 us (6%)
  between operations  15.2 us (4%)
  local copies, waits for them, and re-layouts  7.74 us (2%)
    all_to_all x1, blocking collectives, on_device(): lax.all_to_all(fields, ('pts', 'hrs'), split_axis=1, concat_axis=0, tiled...  101 us
    psum x2, waiting for transfers between devices, on_device(): gram_sum = lax.psum(lax.psum(local_gram, 'hrs'), 'pts')  98.9 us
    psum x1, waiting for transfers between devices, on_device(): lax.psum(contract_last(sketched, panels) / n_points, ('pts', 'hrs'))  71 us
    another operation x6, other arithmetic, on_device(): factor = jnp.linalg.cholesky(gram_sum)  34.2 us
    another operation x4, other arithmetic, on_device(): lax.linalg.triangular_solve(factor, sketched, left_side=True, lower=True)  21.2 us
    dot_general x2, matrix products, contract_last(): lax.dot_general(left, right, (((1,), (1,)), ((), ())), precision=highest,...  9.23 us
  transfers between devices with their start and end apart: 3, of which 3 were waited for; matrix products, arithmetic and copies ran while one was open for 19% of the time, Pallas kernels for 0%

profile of v1, /device:TPU:0, one launch (start us, length us, event | category | flops | bytes accessed | tf_op | source)
XLA Modules:
  0.0 371.8 jit_solution(4214430342743891611)
XLA Ops:
  7.2 2.5 copy.17
  9.7 100.7 %all_to_all.19 = f32[16,32,2048]{2,0,1:T(8,128)S(1)} all-to-all(f32[16,32,2048]{2,0,1:T(8,128)S(1)} %bitcast.50), channel_id=1, replica_groups=mesh['pts'=8,'hrs'=4] {'pts','hrs'}, dimensions={1} | all-to-all | bytes 8388608 | tf_op jit(solution)/shard_map/all_to_all | solution.py:18
  110.5 3.7 fusion.13
  114.2 2.6 convolution_multiply_fusion.1
  116.9 31.4 %all-reduce.5.cloned.1.call-done = f32[256,256]{0,1:T(8,128)} async-done(((f32[256,256]{0,1:T(8,128)}), f32[256,256]{0,1:T(8,128)}) %all-reduce.5.cloned.1.call-update) | async-done | bytes 262160 | tf_op jit(solution)/shard_map/psum | solution.py:23
  148.5 6.7 %convolution_multiply_fusion = f32[256,512]{1,0:T(8,128)} fusion(f32[256,2048]{1,0:T(8,128)S(1)} %fusion.13, f32[512,2048]{1,0:T(8,128)} %bitcast.49), kind=kOutput, calls=%fused_computation.5 | convolution fusion | flops 3221356544 | bytes 6815744 | tf_op jit(solution)/shard_map/dot_general | solution.py:10
  155.2 67.5 %all-reduce.7.cloned.1.call-done = f32[256,256]{0,1:T(8,128)} async-done(((f32[256,256]{0,1:T(8,128)}), f32[256,256]{0,1:T(8,128)}) %all-reduce.7.cloned.1.call-update) | async-done | bytes 262160 | tf_op jit(solution)/shard_map/psum | solution.py:23
  222.7 1.1 copy.13
  223.8 1.0 fusion.4
  224.8 11.7 %cholesky.50 = f32[128,128]{1,0:T(8,128)S(1)} custom-call(f32[128,128]{1,0:T(8,128)S(1)} %cholesky.118), custom_call_target="Cholesky" | custom-call | tf_op jit(solution)/shard_map/jit(cholesky)/cholesky | solution.py:24
  236.5 9.8 %custom-call.16 = f32[1,128,128]{1,2,0:T(8,128)S(1)} custom-call(f32[1,128,128]{2,1,0:T(8,128)S(1)} %get-tuple-element.23), custom_call_target="InvertDiagBlocksLowerTriangular" | custom-call | tf_op jit(solution)/shard_map/jit(cholesky)/cholesky | solution.py:24
  246.9 11.9 %cholesky.105 = f32[128,128]{1,0:T(8,128)S(1)} custom-call(f32[128,128]{1,0:T(8,128)S(1)} %convolution_subtract_fusion.2), custom_call_target="Cholesky" | custom-call | tf_op jit(solution)/shard_map/jit(cholesky)/cholesky | solution.py:24
  260.9 4.1 %while.1 = (s32[]{:T(128)}, f32[256,256]{1,0:T(8,128)S(1)}, s32[2,2]{1,0:T(2,128)S(1)}, f32[2,128,128]{2,1,0:T(8,128)S(1)}, s32[]{:T(128)}) while((s32[]{:T(128)}, f32[256,256]{1,0:T(8,128)S(1)}, s32[2,2]{1,0:T(2,128)S(1)}, f32[2,128,128]{2,1,0:T(8,128)S(1)}, s32[]{:T(128)}) %tuple.27), condition=%wide.while_cond, body=%wide.while_body.sunk | while | flops 2 | bytes 131181 | solution.py:25
  261.6 1.3 bitcast_dynamic-update-slice_fusion.2
  263.6 1.3 bitcast_dynamic-update-slice_fusion.2
  265.0 19.7 %custom-call.17 = f32[2,128,128]{1,2,0:T(8,128)S(1)} custom-call(f32[2,128,128]{2,1,0:T(8,128)S(1)} %get-tuple-element.9), custom_call_target="InvertDiagBlocksLowerTriangular" | custom-call | tf_op jit(solution)/shard_map/triangular_solve | solution.py:25
  284.7 2.0 fusion
  286.7 71.0 %all-reduce.9.cloned.1.call-done = f32[256,512]{1,0:T(8,128)} async-done(((f32[256,512]{1,0:T(8,128)}), f32[256,512]{1,0:T(8,128)}) %all-reduce.9.cloned.1.call-update) | async-done | bytes 524304 | tf_op jit(solution)/shard_map/psum | solution.py:21
  357.6 1.5 fusion.2
  359.1 1.3 convolution_subtract_fusion.1
  360.9 0.8 pad_maximum_fusion.1
  361.7 1.0 convolution_subtract_fusion
  362.7 1.1 fusion.9
  363.8 1.5 pad_maximum_fusion
  (28 shorter events, 3.5 us)
Async XLA Ops:
  7.2 103.3 %copy-start = (f32[256,512]{1,0:T(8,128)S(1)}, f32[256,512]{1,0:T(8,128)}, u32[]{:S(2)}) copy-start(f32[256,512]{1,0:T(8,128)} %param.3) | copy-start | bytes 1572868
  7.2 141.1 %all-reduce.5.cloned.1.call-start = ((), (), s32[]{:S(2)}) async-start(), calls=%async_computation.1 | async-start | bytes 524288 | tf_op jit(solution)/shard_map/psum | solution.py:23
  110.5 3.7 copy-start.1
  116.8 105.9 %all-reduce.7.cloned.1.call-start = ((), (), s32[]{:S(2)}) async-start(), calls=%async_computation.2 | async-start | bytes 524288 | tf_op jit(solution)/shard_map/psum | solution.py:23
  148.3 209.3 %all-reduce.9.cloned.1.call-start = ((), (), s32[]{:S(2)}) async-start(), calls=%async_computation.3 | async-start | bytes 1048576 | tf_op jit(solution)/shard_map/psum | solution.py:21
  357.6 4.1 %copy-start.2 = (f32[128,2048]{1,0:T(8,128)S(1)}, f32[128,2048]{1,0:T(8,128)}, u32[]{:S(2)}) copy-start(f32[128,2048]{1,0:T(8,128)} %fusion) | copy-start | bytes 3145732
Sparse Core Ops, SparseCore 0:
  116.9 31.3 all-reduce.4
  151.6 71.0 all-reduce.6
  228.6 129.0 all-reduce.8
